TPU v7x, 32 devices: a whole 2x2x4 slice. The times are simulated.
32 devices in a mesh: rep: 4 (over z), tp: 8 (over y, x, core).
Axes of the slice: x: 2, y: 2, z: 4, core: 2. Of those that a mesh axis runs over, the one named last changes fastest.
Arguments:
- attn: bfloat16 [3072, 4096], P('rep', 'tp'), parts along dimension 0, may hold values from -6 to 6
- output_weight: bfloat16 [4096, 8192], P(None, 'tp'), may hold values from -0.09375 to 0.09375
- adapter_down_weight: bfloat16 [8, 64, 4096], P('tp'), may hold values from -0.09375 to 0.09375
- adapter_up_weight: bfloat16 [8, 64, 8192], P('tp'), may hold values from -0.75 to 0.75
- block_adapter_index: int32 [24], P('rep'), parts along dimension 0, may hold values from 0 to 7
- adapter_page_table: int32 [8], replicated, may hold values from 0 to 7, each once
Outputs:
- projected: bfloat16 [3072, 8192], P('rep', 'tp'), parts along dimension 0
There are 4 independent parts, one for each index of `rep`. A program takes and returns all parts, laid end to end along the dimension named above; an argument that names none is the same for every part. Nothing has to cross between parts.
Inputs may be any that keep to these rules, and one draw needn't show every extreme that they name: adapter_page_table is a permutation; adapter a is stored on tp device adapter_page_table[a] (each device holds exactly one adapter), and row adapter_page_table[a] of adapter_down_weight and adapter_up_weight holds it. `block_adapter_index`: the adapter used by all 128 tokens of a block.
All inputs are finite; a program needn't handle non-finite values.
Results may differ from a plain program's by a relative error of at most 0.0046.
Values may be sent and summed in bfloat16 or wider, within the bound.
A program may use at most 64 MiB of HBM per device.

v0:
```python
import jax
import jax.numpy as jnp
from jax import lax
from jax.sharding import PartitionSpec as P

adapter_scale = 2.0


def shards(
    attn,
    output_weight,
    adapter_down_weight,
    adapter_up_weight,
    block_adapter_index,
    adapter_page_table,
):
    tokens = attn.shape[0]
    blocks = block_adapter_index.shape[0]
    block_rows = tokens // blocks
    page_slot_count = adapter_down_weight.shape[0]
    pool_size = adapter_page_table.shape[0]
    width_out = output_weight.shape[1]
    position = lax.axis_index("tp")
    matches = block_adapter_index[:, None] == jnp.arange(pool_size, dtype=jnp.int32)[None, :]
    block_page_index = jnp.sum(jnp.where(matches, adapter_page_table[None, :], 0), axis=1)
    up_weight_columns = lax.all_to_all(
        adapter_up_weight, "tp", split_axis=2, concat_axis=0, tiled=True
    )
    block_up = up_weight_columns[block_page_index]
    shard_piece = lax.all_gather(attn, "tp", axis=1, tiled=True)
    base_output = jnp.dot(shard_piece, output_weight, preferred_element_type=jnp.float32)
    row_blocks = shard_piece.reshape(blocks, block_rows, shard_piece.shape[1])
    base_output, side_sum = (
        base_output,
        jnp.einsum(
            "btf,srf->bsrt", row_blocks, adapter_down_weight, preferred_element_type=jnp.float32
        ),
    )
    own_pages = position * page_slot_count + jnp.arange(page_slot_count, dtype=jnp.int32)
    owned = (block_page_index[:, None] == own_pages[None, :]).astype(jnp.float32)
    local_term = jnp.sum(owned[:, :, None, None] * side_sum, axis=1)
    shrunk = lax.psum(local_term.astype(jnp.bfloat16), "tp")
    adapter_output = jnp.einsum(
        "brt,brc->btc", shrunk, block_up, preferred_element_type=jnp.float32
    )
    adapter_output = adapter_output.reshape(tokens, width_out)
    return (base_output + adapter_scale * adapter_output).astype(jnp.bfloat16)


def solution(mesh):
    return jax.shard_map(
        shards,
        mesh=mesh,
        in_specs=(
            P("rep", "tp"),
            P(None, "tp"),
            P("tp", None, None),
            P("tp", None, None),
            P("rep"),
            P(),
        ),
        out_specs=P("rep", "tp"),
        check_vma=False,
    )
```

profile of v0, /device:TPU:0, one launch (start us, length us, event | category | flops | bytes accessed | tf_op | source)
XLA Modules:
  0.0 150.3 jit_solution(16534256131757500711)
XLA Ops:
  6.5 0.0 copy-start
  6.5 0.0 all-gather.2.cloned.1.call-start
  6.5 0.7 all-gather.2.cloned.1.call-update
  7.3 9.2 %copy.11 = bf16[1,64,8192]{1,0,2:T(2,128)(2,1)} copy(bf16[1,64,8192]{2,1,0:T(8,128)(2,1)} %param.9) | data formatting | bytes 2097152 | tf_op args[3]
  16.4 0.5 broadcast.42
  16.9 45.3 %reduce = bf16[8192,64]{1,0:T(8,128)(2,1)S(1)} reduce(bf16[8192,1,64]{2,1,0:T(2,128)(2,1)} %bitcast.36, bf16[]{:T(256)} %broadcast.42), dimensions={1}, to_apply=%bitcast.29.reduce_sub_computation | reduce | bytes 2097154
  62.2 0.0 copy-start.1
  62.2 0.0 copy-start.2
  62.2 2.7 %reshape.51 = bf16[8,2,32768]{2,1,0:T(2,128)(2,1)} reshape(bf16[8192,64]{1,0:T(8,128)(2,1)S(1)} %reduce) | data formatting | bytes 2097152
  64.9 5.2 %all-to-all-start = ((bf16[8,2,32768]{2,1,0:T(2,128)(2,1)}), bf16[8,2,32768]{2,1,0:T(2,128)(2,1)S(1)}, u32[]{:S(2)}, u32[]{:S(2)}) async-start(bf16[8,2,32768]{2,1,0:T(2,128)(2,1)} %reshape.51), calls=%async_computation | async-start | bytes 2097152 | tf_op jit(solution)/shard_map/all_to_all | solution.py:26
  70.1 0.2 all-reduce.2.cloned.1.call-start
  70.3 0.0 copy-done.1
  70.3 0.0 copy-done.2
  70.4 0.2 select_reduce_fusion
  70.6 0.0 all-gather.2.cloned.1.call-done
  70.6 0.0 copy-done
  70.6 5.5 %fusion.3 = bf16[6,64,128]{2,1,0:T(8,128)(2,1)} fusion(bf16[6,128,4096]{2,1,0:T(8,128)(2,1)} %bitcast.39, bf16[1,64,4096]{2,1,0:T(8,128)(2,1)S(1)} %copy-done, f32[6]{0:T(128)S(1)} %compare_convert_fusion), kind=kOutput, calls=%fused_computation.7 | convolution fusion | flops 402751488 | bytes 6914072 | tf_op jit(solution)/shard_map/btf,srf->bsrt/dot_general | solution.py:35
  76.0 0.0 all-reduce.2.cloned.1.call-update
  76.1 9.4 %all-to-all-done = bf16[8,2,32768]{2,1,0:T(2,128)(2,1)S(1)} async-done(((bf16[8,2,32768]{2,1,0:T(2,128)(2,1)}), bf16[8,2,32768]{2,1,0:T(2,128)(2,1)S(1)}, u32[]{:S(2)}, u32[]{:S(2)}) %all-to-all-start) | async-done | bytes 1048608 | tf_op jit(solution)/shard_map/all_to_all | solution.py:26
  85.5 4.3 %reshape.52 = bf16[8192,1,64]{2,1,0:T(2,128)(2,1)} reshape(bf16[8,2,32768]{2,1,0:T(2,128)(2,1)S(1)} %all-to-all-done) | data formatting | bytes 2097152
  89.9 2.5 %copy.16 = bf16[1,64,8192]{1,2,0:T(8,128)(2,1)S(1)} copy(bf16[1,64,8192]{1,0,2:T(2,128)(2,1)} %bitcast.37) | data formatting | bytes 2097152
  92.3 1.6 %copy.13 = bf16[1,64,8,1024]{3,1,2,0:T(8,128)(2,1)} copy(bf16[1,64,8,1024]{1,3,2,0:T(8,128)(2,1)S(1)} %bitcast.38) | data formatting | bytes 2097152 | tf_op jit(solution)/shard_map/all_to_all | solution.py:26
  93.9 1.8 %gather_fusion = bf16[6,64,1024]{2,1,0:T(8,128)(2,1)S(1)} fusion(bf16[8,64,1024]{2,1,0:T(8,128)(2,1)} %bitcast.40, s32[1024]{0:T(1024)S(1)} %pad_clamp_fusion), kind=kCustom, calls=%fused_computation | custom fusion | bytes 1572888 | tf_op jit(solution)/shard_map/gather | solution.py:29
  95.8 34.1 %all-reduce.2.cloned.1.call-done = bf16[6,64,128]{2,1,0:T(8,128)(2,1)} async-done(((bf16[6,64,128]{2,1,0:T(8,128)(2,1)}), bf16[6,64,128]{2,1,0:T(8,128)(2,1)}) %all-reduce.2.cloned.1.call-update) | async-done | bytes 98320 | tf_op jit(solution)/shard_map/psum | solution.py:42
  129.9 1.5 %convolution_multiply_fusion = f32[6,128,1024]{2,1,0:T(8,128)S(1)} fusion(bf16[6,64,128]{2,1,0:T(8,128)(2,1)} %all-reduce.2.cloned.1.call-done, bf16[6,64,1024]{2,1,0:T(8,128)(2,1)S(1)} %gather_fusion), kind=kOutput, calls=%fused_computation.3 | convolution fusion | flops 101449728 | bytes 4030464 | tf_op jit(solution)/shard_map/brt,brc->btc/dot_general | solution.py:43
  131.4 12.1 %fusion = bf16[768,1024]{1,0:T(8,128)(2,1)} fusion(f32[6,128,1024]{2,1,0:T(8,128)S(1)} %convolution_multiply_fusion, bf16[768,4096]{1,0:T(8,128)(2,1)} %all-gather.2.cloned.1.call-done, bf16[4096,1024]{1,0:T(8,128)(2,1)} %param.7), kind=kOutput, calls=%fused_computation.2 | convolution fusion | flops 6444023808 | bytes 19398656 | tf_op jit(solution)/shard_map/dot_general | solution.py:31
  (3 shorter events, 0.0 us)
Async XLA Ops:
  6.5 64.1 %copy-start = (bf16[1,64,4096]{2,1,0:T(8,128)(2,1)S(1)}, bf16[1,64,4096]{2,1,0:T(8,128)(2,1)}, u32[]{:S(2)}) copy-start(bf16[1,64,4096]{2,1,0:T(8,128)(2,1)} %param.8) | copy-start | bytes 1572868
  6.5 64.0 %all-gather.2.cloned.1.call-start = ((), (), s32[]{:S(2)}) async-start(), calls=%async_computation.1 | async-start | bytes 7077888 | tf_op jit(solution)/shard_map/all_gather | solution.py:30
  62.2 8.1 %copy-start.1 = (s32[8]{0:T(128)S(1)}, s32[8]{0:T(128)}, u32[]{:S(2)}) copy-start(s32[8]{0:T(128)} %param.11) | copy-start | bytes 100
  62.2 8.1 %copy-start.2 = (s32[6]{0:T(128)S(1)}, s32[6]{0:T(128)}, u32[]{:S(2)}) copy-start(s32[6]{0:T(128)} %param.10) | copy-start | bytes 76
  64.9 20.6 %all-to-all-start = ((bf16[8,2,32768]{2,1,0:T(2,128)(2,1)}), bf16[8,2,32768]{2,1,0:T(2,128)(2,1)S(1)}, u32[]{:S(2)}, u32[]{:S(2)}) async-start(bf16[8,2,32768]{2,1,0:T(2,128)(2,1)} %reshape.51), calls=%async_computation | async-start | bytes 2097152 | tf_op jit(solution)/shard_map/all_to_all | solution.py:26
  70.1 59.7 %all-reduce.2.cloned.1.call-start = ((), (), s32[]{:S(2)}) async-start(), calls=%async_computation.2 | async-start | bytes 196608 | tf_op jit(solution)/shard_map/psum | solution.py:42
Sparse Core Ops, SparseCore 0:
  9.2 49.2 all-gather.1
  76.2 53.6 all-reduce.1
where the time goes:
time: 151 us; the launch traced here: 150 us
  other arithmetic  45.5 us (30%)
  waiting for transfers between devices  44.3 us (29%)
  local copies, waits for them, and re-layouts  22.6 us (15%)
  matrix products  19.1 us (13%)
  between operations  13.5 us (9%)
  starting transfers between devices  5.45 us (4%)
    unnamed x1, other arithmetic  45.3 us
    psum x1, waiting for transfers between devices, shards(): shrunk = lax.psum(local_term.astype(jnp.bfloat16), 'tp')  34.1 us
    unnamed x11, local copies, waits for them, and re-layouts  19.2 us
    dot_general x1, matrix products, shards(): jnp.dot(shard_piece, output_weight, preferred_element_type=jnp.float32)  12.1 us
    all_to_all x1, waiting for transfers between devices, shards(): lax.all_to_all(adapter_up_weight, 'tp', split_axis=2, concat_axis=0, tile...  9.44 us
    dot_general x1, matrix products, shards(): jnp.einsum('btf,srf->bsrt', row_blocks, adapter_down_weight, preferred_el...  5.45 us
    all_to_all x1, starting transfers between devices, shards(): lax.all_to_all(adapter_up_weight, 'tp', split_axis=2, concat_axis=0, tile...  5.23 us
  transfers between devices with their start and end apart: 3, of which 2 were waited for; matrix products, arithmetic and copies ran while one was open for 49% of the time, Pallas kernels for 0%

commit v1 on v0

v1 whole, which is shorter than its diff:
```python
import functools

import jax
import jax.numpy as jnp
from jax import lax
from jax.experimental import pallas as pl
from jax.experimental.pallas import tpu as pltpu
from jax.sharding import PartitionSpec as P

adapter_scale = 2.0
MESH = pl.DeviceIdType.MESH


def plain_shards(
    attn,
    output_weight,
    adapter_down_weight,
    adapter_up_weight,
    block_adapter_index,
    adapter_page_table,
):
    tokens = attn.shape[0]
    blocks = block_adapter_index.shape[0]
    block_rows = tokens // blocks
    page_slot_count = adapter_down_weight.shape[0]
    width_out = output_weight.shape[1]
    position = lax.axis_index("tp")
    block_page_index = adapter_page_table[block_adapter_index]
    up_weight_columns = lax.all_to_all(
        adapter_up_weight, "tp", split_axis=2, concat_axis=0, tiled=True
    )
    block_up = up_weight_columns[block_page_index]
    gathered = lax.all_gather(attn, "tp", axis=1, tiled=True)
    base_output = jnp.dot(gathered, output_weight, preferred_element_type=jnp.float32)
    row_blocks = gathered.reshape(blocks, block_rows, gathered.shape[1])
    side_sum = jnp.einsum(
        "btf,srf->bsrt", row_blocks, adapter_down_weight, preferred_element_type=jnp.float32
    )
    own_pages = position * page_slot_count + jnp.arange(page_slot_count, dtype=jnp.int32)
    owned = (block_page_index[:, None] == own_pages[None, :]).astype(jnp.float32)
    local_term = jnp.sum(owned[:, :, None, None] * side_sum, axis=1)
    shrunk = lax.psum(local_term.astype(jnp.bfloat16), "tp")
    adapter_output = jnp.einsum(
        "brt,brc->btc", shrunk, block_up, preferred_element_type=jnp.float32
    )
    adapter_output = adapter_output.reshape(tokens, width_out)
    return (base_output + adapter_scale * adapter_output).astype(jnp.bfloat16)


def kernel(
    n,
    reps,
    index_ref,
    table_ref,
    attn_ref,
    weight_ref,
    down_ref,
    up_ref,
    out_ref,
    a_all,
    w_all,
    acc,
    out_stage,
    dn_all,
    up_all,
    part,
    part_in,
    sum_all,
    send_sem,
    recv_sem,
    local_sem,
):
    blocks = index_ref.shape[0]
    rows = a_all.shape[1] // blocks
    rank = dn_all.shape[1]
    f_own = a_all.shape[2]
    c_own = up_all.shape[2]
    share = rank // reps
    red = rank // n
    me = lax.axis_index("tp")
    z = lax.axis_index("rep")
    core = lax.rem(me, 2)
    x_at = lax.rem(me // 2, 2)
    y_at = me // 4
    mate = me + 1 - 2 * core
    xn = me + 2 - 4 * x_at
    yn = me + 4 - 8 * y_at
    dg = xn + 4 - 8 * y_at

    def mate_of(d):
        return d + 1 - 2 * core

    counts = [0, 0]
    sends = []

    def remote(src, dst, axis, target):
        k = counts[0]
        counts[0] += 1
        copy = pltpu.make_async_remote_copy(
            src_ref=src,
            dst_ref=dst,
            send_sem=send_sem.at[k],
            recv_sem=recv_sem.at[k],
            device_id={axis: target},
            device_id_type=MESH,
        )
        copy.start()
        sends.append(copy)
        return copy

    def local(src, dst):
        k = counts[1]
        counts[1] += 1
        copy = pltpu.make_async_copy(src, dst, local_sem.at[k])
        copy.start()
        return copy

    own_load = local(attn_ref, a_all.at[me])
    z_rows = pl.ds(pl.multiple_of(z * share, share), share)
    own_f = pl.ds(pl.multiple_of(me * f_own, f_own), f_own)
    own_c = pl.ds(pl.multiple_of(me * c_own, c_own), c_own)
    own_dn = local(down_ref.at[0, z_rows, own_f], dn_all.at[me, z_rows, :])
    own_up = local(up_ref.at[0, z_rows, own_c], up_all.at[me, z_rows, :])

    barrier = pltpu.get_barrier_semaphore()
    for d in range(1, n):
        pl.semaphore_signal(
            barrier, inc=1, device_id={"tp": lax.rem(me + d, n)}, device_id_type=MESH
        )
    for d in range(1, reps):
        pl.semaphore_signal(
            barrier, inc=1, device_id={"rep": lax.rem(z + d, reps)}, device_id_type=MESH
        )
    pl.semaphore_wait(barrier, n - 1 + reps - 1)

    dn_copies, up_copies = [], []
    for d in range(1, n):
        j = lax.rem(me + d, n)
        cols = pl.ds(pl.multiple_of(j * f_own, f_own), f_own)
        dn_copies.append(
            remote(down_ref.at[0, z_rows, cols], dn_all.at[me, z_rows, :], "tp", j)
        )
    for d in range(1, n):
        j = lax.rem(me + d, n)
        cols = pl.ds(pl.multiple_of(j * c_own, c_own), c_own)
        up_copies.append(
            remote(up_ref.at[0, z_rows, cols], up_all.at[me, z_rows, :], "tp", j)
        )

    own_load.wait()

    def chunk(slot, b):
        return a_all.at[slot, pl.ds(b * rows, rows), :]

    x_copies = []
    y_copies = []
    mate_copy = remote(a_all.at[me], a_all.at[me], "tp", mate)
    for b in range(blocks):
        x_copies.append(remote(chunk(me, b), chunk(me, b), "tp", xn))
        y_copies.append(remote(chunk(me, b), chunk(me, b), "tp", yn))

    w_loads = [local(weight_ref.at[pl.ds(pl.multiple_of(s * f_own, f_own), f_own), :], w_all.at[s])
               for s in (me, mate, xn, mate_of(xn), yn, mate_of(yn), dg, mate_of(dg))]

    own_dn.wait()
    for copy in dn_copies:
        copy.wait_recv()
    dn_z = [
        remote(dn_all.at[:, z_rows, :], dn_all.at[:, z_rows, :], "rep", lax.rem(z + d, reps))
        for d in range(1, reps)
    ]
    own_up.wait()
    for copy in up_copies:
        copy.wait_recv()
    up_z = [
        remote(up_all.at[:, z_rows, :], up_all.at[:, z_rows, :], "rep", lax.rem(z + d, reps))
        for d in range(1, reps)
    ]

    width = acc.shape[1]
    tile = 256

    def multiply(first, size, slots, fresh):
        at = pl.ds(first, size)

        @pl.loop(0, width // tile)
        def _(t):
            cols = pl.ds(pl.multiple_of(t * tile, tile), tile)
            total = None
            for s in slots:
                term = jnp.dot(
                    a_all[s, at, :], w_all[s, :, cols], preferred_element_type=jnp.float32
                )
                total = term if total is None else total + term
            if fresh:
                acc[at, cols] = total
            else:
                acc[at, cols] += total

    pair = 2 * rows
    mate_copy.wait_recv()
    w_loads[0].wait()
    w_loads[1].wait()
    for s in range(blocks // 2):
        multiply(s * pair, pair, (me, mate), True)

    def pages(b):
        return table_ref[index_ref[b]]

    def shrink():
        for copy in dn_z:
            copy.wait_recv()
        for b in range(blocks):
            part[b] = lax.dot_general(
                dn_all[pages(b)],
                a_all[me, pl.ds(b * rows, rows), :],
                (((1,), (1,)), ((), ())),
                preferred_element_type=jnp.float32,
            )
        copies = []
        for d in range(1, n):
            j = lax.rem(me + d, n)
            copies.append(
                remote(
                    part.at[:, pl.ds(pl.multiple_of(j * red, red), red), :],
                    part_in.at[d - 1],
                    "tp",
                    j,
                )
            )
        return copies

    def reduce(copies):
        mine = pl.ds(pl.multiple_of(me * red, red), red)
        total = part[:, mine, :]
        for d in range(1, n):
            copies[d - 1].wait_recv()
            total = total + part_in[d - 1]
        sum_all[:, mine, :] = total
        return [
            remote(sum_all.at[:, mine, :], sum_all.at[:, mine, :], "tp", lax.rem(me + d, n))
            for d in range(1, n)
        ]

    x_mate, y_mate, dg_copies = [], [], []
    for s in range(blocks // 2):
        for b in (2 * s, 2 * s + 1):
            x_copies[b].wait_recv()
            if b % 2 == 1:
                dg_copies.append(remote(chunk(xn, b), chunk(xn, b), "tp", yn))
            x_mate.append(remote(chunk(xn, b), chunk(xn, b), "tp", mate))
            y_copies[b].wait_recv()
            if b % 2 == 0:
                dg_copies.append(remote(chunk(yn, b), chunk(yn, b), "tp", xn))
            y_mate.append(remote(chunk(yn, b), chunk(yn, b), "tp", mate))
        if s == 0:
            for load in w_loads[2:6]:
                load.wait()
        x_mate[2 * s].wait_recv()
        x_mate[2 * s + 1].wait_recv()
        y_mate[2 * s].wait_recv()
        y_mate[2 * s + 1].wait_recv()
        multiply(s * pair, pair, (xn, mate_of(xn), yn, mate_of(yn)), False)
        if s == blocks // 2 - 2:
            part_copies = shrink()
    sum_copies = reduce(part_copies)

    w_loads[6].wait()
    w_loads[7].wait()
    dg_mate = []
    out_copies = []
    for s in range(blocks // 2):
        for b in (2 * s, 2 * s + 1):
            dg_copies[b].wait_recv()
            dg_mate.append(remote(chunk(dg, b), chunk(dg, b), "tp", mate))
        if s == 0:
            for copy in sum_copies:
                copy.wait_recv()
            for copy in up_z:
                copy.wait_recv()
        for b in (2 * s, 2 * s + 1):
            low = sum_all[b].astype(jnp.bfloat16)
            page = pages(b)
            at = pl.ds(b * rows, rows)
            adapted = lax.dot_general(
                low, up_all[page], (((0,), (0,)), ((), ())), preferred_element_type=jnp.float32
            )
            acc[at, :] += adapter_scale * adapted
        dg_mate[2 * s].wait_recv()
        dg_mate[2 * s + 1].wait_recv()
        at = pl.ds(s * pair, pair)

        @pl.loop(0, width // tile)
        def _(t):
            cols = pl.ds(pl.multiple_of(t * tile, tile), tile)
            total = acc[at, cols]
            for slot in (dg, mate_of(dg)):
                total = total + jnp.dot(
                    a_all[slot, at, :], w_all[slot, :, cols], preferred_element_type=jnp.float32
                )
            out_stage[at, cols] = total.astype(out_stage.dtype)

        out_copies.append(local(out_stage.at[at, :], out_ref.at[at, :]))

    for copy in sends:
        copy.wait_send()
    for copy in out_copies:
        copy.wait()


def shards(n, reps, attn, weight, down, up, index, table):
    tokens, f_own = attn.shape
    blocks = index.shape[0]
    rows = tokens // blocks
    features, width = weight.shape
    rank = down.shape[1]
    copies = 2 * (n - 1) + 1 + 2 * blocks + 2 * (reps - 1) + 4 * blocks + 2 * (n - 1)
    return pl.pallas_call(
        functools.partial(kernel, n, reps),
        out_shape=jax.ShapeDtypeStruct((tokens, width), jnp.bfloat16),
        in_specs=[pl.BlockSpec(memory_space=pltpu.SMEM)] * 2
        + [pl.BlockSpec(memory_space=pl.ANY)] * 4,
        out_specs=pl.BlockSpec(memory_space=pl.ANY),
        scratch_shapes=[
            pltpu.VMEM((n, tokens, f_own), jnp.bfloat16),
            pltpu.VMEM((n, features // n, width), jnp.bfloat16),
            pltpu.VMEM((tokens, width), jnp.float32),
            pltpu.VMEM((tokens, width), jnp.bfloat16),
            pltpu.VMEM((n, rank, f_own), jnp.bfloat16),
            pltpu.VMEM((n, rank, width), jnp.bfloat16),
            pltpu.VMEM((blocks, rank, rows), jnp.float32),
            pltpu.VMEM((n - 1, blocks, rank // n, rows), jnp.float32),
            pltpu.VMEM((blocks, rank, rows), jnp.float32),
            pltpu.SemaphoreType.DMA((copies,)),
            pltpu.SemaphoreType.DMA((copies,)),
            pltpu.SemaphoreType.DMA((3 + n + blocks // 2,)),
        ],
        compiler_params=pltpu.CompilerParams(
            collective_id=0, has_side_effects=True, vmem_limit_bytes=60 * 1024 * 1024
        ),
    )(index, table, attn, weight, down, up)


def solution(mesh):
    n, reps = mesh.shape["tp"], mesh.shape["rep"]

    def body(attn, weight, down, up, index, table):
        blocks = index.shape[0]
        fits = (
            n == 8
            and reps > 1
            and blocks % 2 == 0
            and blocks >= 4
            and down.shape[0] == 1
            and down.shape[1] % (16 * reps) == 0
            and down.shape[1] % (8 * n) == 0
            and attn.shape[0] % (128 * blocks) == 0
            and attn.shape[1] % 128 == 0
            and weight.shape[1] % 256 == 0
        )
        if fits:
            return shards(n, reps, attn, weight, down, up, index, table)
        return plain_shards(attn, weight, down, up, index, table)

    return jax.shard_map(
        body,
        mesh=mesh,
        in_specs=(
            P("rep", "tp"),
            P(None, "tp"),
            P("tp", None, None),
            P("tp", None, None),
            P("rep"),
            P(),
        ),
        out_specs=P("rep", "tp"),
        check_vma=False,
    )
```

time: 151 us -> 55.7 us (0.37)
  the two profiles are of different devices: /device:TPU:0 before, /device:TPU:9 now
where the time goes in v1:
time: 55.7 us; the launch traced here: 55.6 us
  Pallas kernels  52.9 us (95%)
  local copies, waits for them, and re-layouts  2.67 us (5%)
    pallas_call x1, Pallas kernels, shards(): pl.pallas_call(functools.partial(kernel, n, reps), out_shape=jax.ShapeDty...  52.9 us
    unnamed x1, local copies, waits for them, and re-layouts  2.67 us

profile of v1, /device:TPU:9, one launch (start us, length us, event | category | flops | bytes accessed | tf_op | source)
XLA Modules:
  0.0 55.6 jit_solution(6547631852187765950)
XLA Ops:
  0.0 52.9 %shard_map.64 = bf16[768,1024]{1,0:T(8,128)(2,1)} custom-call(s32[6]{0:T(128)} %index_ref.1, s32[8]{0:T(128)} %table_ref.1, bf16[768,512]{1,0:T(8,128)(2,1)} %attn_ref.1, bf16[4096,1024]{1,0:T(8,128)(2,1)} %weight_ref.1, bf16[1,64,4096]{2,1,0:T(8,128)(2,1)} %down_ref.1, bf16[1,64,8192]{2,1,0:T(8,128)(2,1)} %up_ref.1), custom_call_target="tpu_custom_call" | custom-call | tf_op jit(solution)/shard_map/pallas_call | solution.py:318
  52.9 2.7 %copy.8 = bf16[768,1024]{1,0:T(8,128)(2,1)} copy(bf16[768,1024]{1,0:T(8,128)(2,1)} %shard_map.64) | data formatting | bytes 3145728

commit v2 on v1

v2 whole, which is shorter than its diff:
```python
import functools

import jax
import jax.numpy as jnp
from jax import lax
from jax.experimental import pallas as pl
from jax.experimental.pallas import tpu as pltpu
from jax.sharding import PartitionSpec as P

adapter_scale = 2.0
MESH = pl.DeviceIdType.MESH


def plain_shards(
    attn,
    output_weight,
    adapter_down_weight,
    adapter_up_weight,
    block_adapter_index,
    adapter_page_table,
):
    tokens = attn.shape[0]
    blocks = block_adapter_index.shape[0]
    block_rows = tokens // blocks
    page_slot_count = adapter_down_weight.shape[0]
    width_out = output_weight.shape[1]
    position = lax.axis_index("tp")
    block_page_index = adapter_page_table[block_adapter_index]
    up_weight_columns = lax.all_to_all(
        adapter_up_weight, "tp", split_axis=2, concat_axis=0, tiled=True
    )
    block_up = up_weight_columns[block_page_index]
    gathered = lax.all_gather(attn, "tp", axis=1, tiled=True)
    base_output = jnp.dot(gathered, output_weight, preferred_element_type=jnp.float32)
    row_blocks = gathered.reshape(blocks, block_rows, gathered.shape[1])
    side_sum = jnp.einsum(
        "btf,srf->bsrt", row_blocks, adapter_down_weight, preferred_element_type=jnp.float32
    )
    own_pages = position * page_slot_count + jnp.arange(page_slot_count, dtype=jnp.int32)
    owned = (block_page_index[:, None] == own_pages[None, :]).astype(jnp.float32)
    local_term = jnp.sum(owned[:, :, None, None] * side_sum, axis=1)
    shrunk = lax.psum(local_term.astype(jnp.bfloat16), "tp")
    adapter_output = jnp.einsum(
        "brt,brc->btc", shrunk, block_up, preferred_element_type=jnp.float32
    )
    adapter_output = adapter_output.reshape(tokens, width_out)
    return (base_output + adapter_scale * adapter_output).astype(jnp.bfloat16)


depth = 3


def link_orders(blocks):
    x_order, y_order = [(False, 1), (False, 0), (False, 3)], [(False, 0), (False, 1), (False, 2)]
    for s in range(blocks // 2):
        x_order.append((True, 2 * s))
        y_order.append((True, 2 * s + 1))
        for order, b in ((x_order, 2 * s + 2), (x_order, 2 * s + 5), (y_order, 2 * s + 3), (y_order, 2 * s + 4)):
            if b < blocks:
                order.append((False, b))
    return x_order, y_order


def kernel(
    n,
    reps,
    index_ref,
    table_ref,
    attn_ref,
    weight_ref,
    down_ref,
    up_ref,
    out_ref,
    a_all,
    w_all,
    acc,
    out_stage,
    dn_all,
    up_all,
    part,
    half_in,
    chip_part,
    part_in,
    sum_all,
    send_sem,
    recv_sem,
    local_sem,
):
    blocks = index_ref.shape[0]
    rows = a_all.shape[1] // blocks
    rank = dn_all.shape[1]
    f_own = a_all.shape[2]
    c_own = up_all.shape[2]
    share = rank // reps
    red = rank // n
    me = lax.axis_index("tp")
    z = lax.axis_index("rep")
    core = lax.rem(me, 2)
    x_at = lax.rem(me // 2, 2)
    y_at = me // 4
    mate = me + 1 - 2 * core
    xn = me + 2 - 4 * x_at
    yn = me + 4 - 8 * y_at
    dg = xn + 4 - 8 * y_at

    def mate_of(d):
        return d + 1 - 2 * core

    counts = [0, 0]
    sends = []

    def remote(src, dst, axis, target):
        k = counts[0]
        counts[0] += 1
        copy = pltpu.make_async_remote_copy(
            src_ref=src,
            dst_ref=dst,
            send_sem=send_sem.at[k],
            recv_sem=recv_sem.at[k],
            device_id={axis: target},
            device_id_type=MESH,
        )
        copy.start()
        sends.append(copy)
        return copy

    def local(src, dst):
        k = counts[1]
        counts[1] += 1
        copy = pltpu.make_async_copy(src, dst, local_sem.at[k])
        copy.start()
        return copy

    own_load = local(attn_ref, a_all.at[me])
    z_rows = pl.ds(pl.multiple_of(z * share, share), share)
    own_f = pl.ds(pl.multiple_of(me * f_own, f_own), f_own)
    own_c = pl.ds(pl.multiple_of(me * c_own, c_own), c_own)
    own_dn = local(down_ref.at[0, :, own_f], dn_all.at[me])
    own_up = local(up_ref.at[0, z_rows, own_c], up_all.at[me, z_rows, :])

    barrier = pltpu.get_barrier_semaphore()
    for d in range(1, n):
        pl.semaphore_signal(
            barrier, inc=1, device_id={"tp": lax.rem(me + d, n)}, device_id_type=MESH
        )
    for d in range(1, reps):
        pl.semaphore_signal(
            barrier, inc=1, device_id={"rep": lax.rem(z + d, reps)}, device_id_type=MESH
        )
    pl.semaphore_wait(barrier, n - 1 + reps - 1)

    dn_copies, up_copies = [], []
    for d in range(1, n):
        j = lax.rem(me + d, n)
        cols = pl.ds(pl.multiple_of(j * f_own, f_own), f_own)
        dn_copies.append(
            remote(down_ref.at[0, :, cols], dn_all.at[me], "tp", j)
        )
    for d in range(1, n):
        j = lax.rem(me + d, n)
        cols = pl.ds(pl.multiple_of(j * c_own, c_own), c_own)
        up_copies.append(
            remote(up_ref.at[0, z_rows, cols], up_all.at[me, z_rows, :], "tp", j)
        )

    own_load.wait()

    def chunk(slot, b):
        return a_all.at[slot, pl.ds(b * rows, rows), :]

    x_order, y_order = link_orders(blocks)
    x_copies, y_copies, x_mate, y_mate = [], [], {}, {}

    def issue(k):
        if k < len(x_order):
            passed, b = x_order[k]
            slot = yn if passed else me
            x_copies.append(remote(chunk(slot, b), chunk(slot, b), "tp", xn))
            passed, b = y_order[k]
            slot = xn if passed else me
            y_copies.append(remote(chunk(slot, b), chunk(slot, b), "tp", yn))

    def event(k):
        x_copies[k].wait_recv()
        y_copies[k].wait_recv()
        issue(k + depth)
        passed, b = x_order[k]
        slot = dg if passed else xn
        x_mate[passed, b] = remote(chunk(slot, b), chunk(slot, b), "tp", mate)
        passed, b = y_order[k]
        slot = dg if passed else yn
        y_mate[passed, b] = remote(chunk(slot, b), chunk(slot, b), "tp", mate)

    issue(0)
    mate_copy = remote(a_all.at[me], a_all.at[me], "tp", mate)
    issue(1)

    w_loads = [local(weight_ref.at[pl.ds(pl.multiple_of(s * f_own, f_own), f_own), :], w_all.at[s])
               for s in (me, mate, xn, mate_of(xn), yn, mate_of(yn), dg, mate_of(dg))]

    width = acc.shape[1]
    tile = 256
    pair = 2 * rows
    pairs = blocks // 2

    def multiply(s, slots, fresh=False):
        at = pl.ds(s * pair, pair)

        @pl.loop(0, width // tile)
        def _(t):
            cols = pl.ds(pl.multiple_of(t * tile, tile), tile)
            total = None if fresh else acc[at, cols]
            for slot in slots:
                term = jnp.dot(
                    a_all[slot, at, :], w_all[slot, :, cols], preferred_element_type=jnp.float32
                )
                total = term if total is None else total + term
            acc[at, cols] = total

    def multiply_sides(s):
        for b in (2 * s, 2 * s + 1):
            x_mate[False, b].wait_recv()
            y_mate[False, b].wait_recv()
        multiply(s, (xn, mate_of(xn), yn, mate_of(yn)))

    def multiply_diagonal(s):
        x_mate[True, 2 * s].wait_recv()
        y_mate[True, 2 * s + 1].wait_recv()
        multiply(s, (dg, mate_of(dg)))

    half = rank // 2
    my_half = pl.ds(pl.multiple_of(core * half, half), half)
    mate_half = pl.ds(pl.multiple_of((1 - core) * half, half), half)

    def piece(device):
        return pl.ds(pl.multiple_of(core * half + (device // 2) * red, red), red)

    peers = (xn, yn, dg)

    def pages(b):
        return table_ref[index_ref[b]]

    own_dn.wait()
    for copy in dn_copies:
        copy.wait_recv()
    for b in range(blocks):
        part[b] = lax.dot_general(
            dn_all[pages(b)],
            a_all[me, pl.ds(b * rows, rows), :],
            (((1,), (1,)), ((), ())),
            preferred_element_type=jnp.float32,
        )
    half_copy = remote(part.at[:, mate_half, :], half_in, "tp", mate)
    mate_copy.wait_recv()
    w_loads[0].wait()
    w_loads[1].wait()
    multiply(0, (me, mate), True)
    half_copy.wait_recv()
    chip_part[:, my_half, :] = part[:, my_half, :] + half_in[...]
    part_copies = [
        remote(chip_part.at[:, piece(p), :], part_in.at[i], "tp", p) for i, p in enumerate(peers)
    ]
    issue(2)
    own_up.wait()
    for copy in up_copies:
        copy.wait_recv()
    up_z = [
        remote(up_all.at[:, z_rows, :], up_all.at[:, z_rows, :], "rep", lax.rem(z + d, reps))
        for d in range(1, reps)
    ]
    event(0)
    multiply(1, (me, mate), True)
    event(1)
    for s in range(2, pairs):
        multiply(s, (me, mate), True)
    for load in w_loads[2:]:
        load.wait()
    event(2)
    total = chip_part[:, piece(me), :]
    for i in range(len(peers)):
        part_copies[i].wait_recv()
        total = total + part_in[i]
    sum_all[:, piece(me), :] = total
    sum_copies = [
        remote(sum_all.at[:, piece(me), :], sum_all.at[:, piece(me), :], "tp", p) for p in peers
    ]
    multiply_sides(0)

    event(3)
    event(4)
    multiply_sides(1)
    event(5)
    multiply_diagonal(0)
    event(6)
    for copy in sum_copies:
        copy.wait_recv()
    sum_mate = remote(sum_all.at[:, my_half, :], sum_all.at[:, my_half, :], "tp", mate)
    multiply_diagonal(1)
    event(7)
    sum_mate.wait_recv()
    for copy in up_z:
        copy.wait_recv()
    for b in range(blocks):
        at = pl.ds(b * rows, rows)
        adapted = lax.dot_general(
            sum_all[b].astype(jnp.bfloat16),
            up_all[pages(b)],
            (((0,), (0,)), ((), ())),
            preferred_element_type=jnp.float32,
        )
        acc[at, :] += adapter_scale * adapted
    multiply_sides(pairs - 1)
    out_copies = []
    for s in range(pairs - 1):
        at = pl.ds(s * pair, pair)
        out_stage[at, :] = acc[at, :].astype(out_stage.dtype)
        out_copies.append(local(out_stage.at[at, :], out_ref.at[at, :]))
    event(8)
    last = pairs - 1
    multiply(last, (dg,))
    x_mate[True, 2 * last].wait_recv()
    y_mate[True, 2 * last + 1].wait_recv()
    at = pl.ds(last * pair, pair)

    @pl.loop(0, width // tile)
    def _(t):
        cols = pl.ds(pl.multiple_of(t * tile, tile), tile)
        slot = mate_of(dg)
        total = acc[at, cols] + jnp.dot(
            a_all[slot, at, :], w_all[slot, :, cols], preferred_element_type=jnp.float32
        )
        out_stage[at, cols] = total.astype(out_stage.dtype)

    out_copies.append(local(out_stage.at[at, :], out_ref.at[at, :]))
    for copy in sends:
        copy.wait_send()
    for copy in out_copies:
        copy.wait()


def shards(n, reps, attn, weight, down, up, index, table):
    tokens, f_own = attn.shape
    blocks = index.shape[0]
    rows = tokens // blocks
    features, width = weight.shape
    rank = down.shape[1]
    copies = 2 * (n - 1) + 1 + 3 * blocks + (reps - 1) + 3 * blocks + 2 * (n // 2 - 1) + 2
    return pl.pallas_call(
        functools.partial(kernel, n, reps),
        out_shape=jax.ShapeDtypeStruct((tokens, width), jnp.bfloat16),
        in_specs=[pl.BlockSpec(memory_space=pltpu.SMEM)] * 2
        + [pl.BlockSpec(memory_space=pl.ANY)] * 4,
        out_specs=pl.BlockSpec(memory_space=pl.ANY),
        scratch_shapes=[
            pltpu.VMEM((n, tokens, f_own), jnp.bfloat16),
            pltpu.VMEM((n, features // n, width), jnp.bfloat16),
            pltpu.VMEM((tokens, width), jnp.float32),
            pltpu.VMEM((tokens, width), jnp.bfloat16),
            pltpu.VMEM((n, rank, f_own), jnp.bfloat16),
            pltpu.VMEM((n, rank, width), jnp.bfloat16),
            pltpu.VMEM((blocks, rank, rows), jnp.float32),
            pltpu.VMEM((blocks, rank // 2, rows), jnp.float32),
            pltpu.VMEM((blocks, rank, rows), jnp.float32),
            pltpu.VMEM((n // 2 - 1, blocks, rank // n, rows), jnp.float32),
            pltpu.VMEM((blocks, rank, rows), jnp.float32),
            pltpu.SemaphoreType.DMA((copies,)),
            pltpu.SemaphoreType.DMA((copies,)),
            pltpu.SemaphoreType.DMA((3 + n + blocks // 2,)),
        ],
        compiler_params=pltpu.CompilerParams(
            collective_id=0, has_side_effects=True, vmem_limit_bytes=60 * 1024 * 1024
        ),
    )(index, table, attn, weight, down, up)


def solution(mesh):
    n, reps = mesh.shape["tp"], mesh.shape["rep"]

    def body(attn, weight, down, up, index, table):
        blocks = index.shape[0]
        fits = (
            n == 8
            and reps > 1
            and blocks % 2 == 0
            and blocks == 6
            and down.shape[0] == 1
            and down.shape[1] % (16 * reps) == 0
            and down.shape[1] % (8 * n) == 0
            and attn.shape[0] % (128 * blocks) == 0
            and attn.shape[1] % 128 == 0
            and weight.shape[1] % 256 == 0
        )
        if fits:
            return shards(n, reps, attn, weight, down, up, index, table)
        return plain_shards(attn, weight, down, up, index, table)

    return jax.shard_map(
        body,
        mesh=mesh,
        in_specs=(
            P("rep", "tp"),
            P(None, "tp"),
            P("tp", None, None),
            P("tp", None, None),
            P("rep"),
            P(),
        ),
        out_specs=P("rep", "tp"),
        check_vma=False,
    )
```

time: 55.7 us -> 52.5 us (0.943)
  the two profiles are of different devices: /device:TPU:9 before, /device:TPU:0 now
where the time goes in v2:
time: 52.5 us; the launch traced here: 52.3 us
  Pallas kernels  49.6 us (94%)
  local copies, waits for them, and re-layouts  2.67 us (5%)
    pallas_call x1, Pallas kernels, shards(): pl.pallas_call(functools.partial(kernel, n, reps), out_shape=jax.ShapeDty...  49.6 us
    unnamed x1, local copies, waits for them, and re-layouts  2.67 us

profile of v2, /device:TPU:0, one launch (start us, length us, event | category | flops | bytes accessed | tf_op | source)
XLA Modules:
  0.0 52.3 jit_solution(14367214812615805115)
XLA Ops:
  0.0 49.6 %shard_map.64 = bf16[768,1024]{1,0:T(8,128)(2,1)} custom-call(s32[6]{0:T(128)} %index_ref.1, s32[8]{0:T(128)} %table_ref.1, bf16[768,512]{1,0:T(8,128)(2,1)} %attn_ref.1, bf16[4096,1024]{1,0:T(8,128)(2,1)} %weight_ref.1, bf16[1,64,4096]{2,1,0:T(8,128)(2,1)} %down_ref.1, bf16[1,64,8192]{2,1,0:T(8,128)(2,1)} %up_ref.1), custom_call_target="tpu_custom_call" | custom-call | tf_op jit(solution)/shard_map/pallas_call | solution.py:348
  49.6 2.7 %copy.8 = bf16[768,1024]{1,0:T(8,128)(2,1)} copy(bf16[768,1024]{1,0:T(8,128)(2,1)} %shard_map.64) | data formatting | bytes 3145728
